TPU v7x, 32 devices: a whole 2x2x4 slice. The times are simulated.
32 devices in a mesh: lat: 16 (over z, x, core), lon: 2 (over y).
Axes of the slice: x: 2, y: 2, z: 4, core: 2. Of those that a mesh axis runs over, the one named last changes fastest.
Arguments:
- elevation: float32 [4096, 4096], P('lat', 'lon'), may hold values from -200 to 200
Outputs:
- slope_angle: float32 [4096, 4096], P('lat', 'lon')
- facing: float32 [2, 4096, 4096], P(None, 'lat', 'lon')
- hillshade: float32 [4096, 4096], P('lat', 'lon')
All inputs are finite; a program needn't handle non-finite values.
Results may differ from a plain program's by a relative error of at most 0.0003.
Values sent between devices are 32-bit elements; how exact they have to be, the bound alone decides.
A program may use at most 64 MiB of HBM per device.

v0:
```python
import math

import jax
import jax.numpy as jnp
from jax import lax
from jax.sharding import PartitionSpec as P

SCALES = 7
HALO = 64


LIGHT_EAST = -0.5
LIGHT_NORTH = 0.5
LIGHT_UP = math.sqrt(0.5)


def padded_2(block, sides, width, periodic):
    for axis, dim in sides:
        count = lax.axis_size(axis)
        forward = [(i, i + 1) for i in range(count - 1)]
        if periodic:
            forward.append((count - 1, 0))
        backward = [(target, source) for source, target in forward]
        low = lax.ppermute(
            lax.slice_in_dim(block, block.shape[dim] - width, None, axis=dim), axis, forward
        )
        high = lax.ppermute(lax.slice_in_dim(block, 0, width, axis=dim), axis, backward)
        block = jnp.concatenate([low, block, high], axis=dim)
    return block


def window(padded, margin, row_offset, col_offset, row_count, col_count):
    return lax.slice(
        padded,
        (margin + row_offset, margin + col_offset),
        (margin + row_offset + row_count, margin + col_offset + col_count),
    )


def terrain_shading(padded, spacing, margin, levels):
    row_count = padded.shape[0] - 2 * margin
    col_count = padded.shape[1] - 2 * margin
    eastward = jnp.zeros((row_count, col_count), jnp.float32)
    northward = jnp.zeros((row_count, col_count), jnp.float32)
    for octave in range(levels):
        stride = 2**octave
        north_west = window(padded, margin, -stride, -stride, row_count, col_count)
        north_mid = window(padded, margin, -stride, 0, row_count, col_count)
        north_east = window(padded, margin, -stride, stride, row_count, col_count)
        west_mid = window(padded, margin, 0, -stride, row_count, col_count)
        east_mid = window(padded, margin, 0, stride, row_count, col_count)
        south_west = window(padded, margin, stride, -stride, row_count, col_count)
        south_mid = window(padded, margin, stride, 0, row_count, col_count)
        south_east = window(padded, margin, stride, stride, row_count, col_count)
        east_diff = (
            north_east + 2.0 * east_mid + south_east - (north_west + 2.0 * west_mid + south_west)
        )
        north_diff = (
            north_west + 2.0 * north_mid + north_east - (south_west + 2.0 * south_mid + south_east)
        )
        eastward = eastward + east_diff * (1.0 / stride)
        northward = northward + north_diff * (1.0 / stride)
    grad_east = eastward / (8.0 * levels * spacing[:, None])
    grad_north = northward * (1.0 / (8.0 * levels))
    squared = grad_east * grad_east + grad_north * grad_north
    slope_angle = jnp.arctan(jnp.sqrt(squared))
    inverse = lax.rsqrt(1.0 + squared)
    facing_east = -grad_east * inverse
    facing_north = -grad_north * inverse
    shading = jnp.maximum(
        LIGHT_EAST * facing_east + LIGHT_NORTH * facing_north + LIGHT_UP * inverse, 0.0
    )
    return (slope_angle, jnp.stack([facing_east, facing_north]), shading)


def pole_clamp(padded, margin):
    lat_index = lax.axis_index("lat")
    last_index = lax.axis_size("lat") - 1
    padded_rows = padded.shape[0]
    position = lax.broadcasted_iota(jnp.int32, (padded_rows, 1), 0)
    top_row = padded[margin : margin + 1]
    bottom_row = padded[padded_rows - margin - 1 : padded_rows - margin]
    above = jnp.logical_and(position < margin, lat_index == 0)
    below = jnp.logical_and(position >= padded_rows - margin, lat_index == last_index)
    return jnp.where(above, top_row, jnp.where(below, bottom_row, padded))


def with_rims(elevation, margin):
    broad_tile = padded_2(elevation, (("lon", 1),), margin, True)
    broad_tile = padded_2(broad_tile, (("lat", 0),), margin, False)
    return pole_clamp(broad_tile, margin)


def local(elevation):
    row_count, col_count = elevation.shape
    total_rows = row_count * lax.axis_size("lat")
    total_cols = col_count * lax.axis_size("lon")
    margin = HALO
    position = lax.axis_index("lat") * row_count + lax.iota(jnp.int32, row_count)
    spacing = jnp.sin((position.astype(jnp.float32) + 0.5) * (math.pi / total_rows)) * (
        2.0 * total_rows / total_cols
    )
    padded = with_rims(elevation, margin)
    return terrain_shading(padded, spacing, margin, SCALES)


def solution(mesh):
    in_specs = (P("lat", "lon"),)
    out_specs = (P("lat", "lon"), P(None, "lat", "lon"), P("lat", "lon"))
    return jax.shard_map(local, mesh=mesh, in_specs=in_specs, out_specs=out_specs, check_vma=False)
```

profile of v0, /device:TPU:9, one launch (start us, length us, event | category | flops | bytes accessed | tf_op | source)
XLA Modules:
  0.0 68.1 jit_solution(1316667555564179711)
XLA Ops:
  0.6 1.1 %fusion.104 = (f32[256,64]{1,0:T(8,128)S(1)}, f32[256,64]{1,0:T(8,128)S(1)}) fusion(f32[256,2048]{1,0:T(8,128)} %param.1), kind=kLoop, calls=%fused_computation.143 | loop fusion | bytes 262144 | tf_op jit(solution)/shard_map/slice | solution.py:27
  1.7 1.3 %collective-permute-start.1 = (f32[256,64]{1,0:T(8,128)S(1)}, f32[256,64]{1,0:T(8,128)S(1)}, u32[]{:S(2)}, u32[]{:S(2)}) collective-permute-start(f32[256,64]{1,0:T(8,128)S(1)} %get-tuple-element.13), channel_id=1, source_target_pairs={{1,0},{0,1},{3,2},{2,3},{5,4},{4,5},{7,6},{6,7},{9,8},{8,9},{11,10... | collective-permute-start | bytes 196616 | tf_op jit(solution)/shard_map/ppermute | solution.py:27
  3.0 0.2 collective-permute-start
  3.2 2.9 %collective-permute-done.1 = f32[256,64]{1,0:T(8,128)S(1)} collective-permute-done((f32[256,64]{1,0:T(8,128)S(1)}, f32[256,64]{1,0:T(8,128)S(1)}, u32[]{:S(2)}, u32[]{:S(2)}) %collective-permute-start.1) | collective-permute-done | bytes 65568 | tf_op jit(solution)/shard_map/ppermute | solution.py:27
  6.1 2.8 %collective-permute-done = f32[256,64]{1,0:T(8,128)S(1)} collective-permute-done((f32[256,64]{1,0:T(8,128)S(1)}, f32[256,64]{1,0:T(8,128)S(1)}, u32[]{:S(2)}, u32[]{:S(2)}) %collective-permute-start) | collective-permute-done | bytes 65568 | tf_op jit(solution)/shard_map/ppermute | solution.py:24
  9.0 3.0 %concatenate.6 = f32[256,2176]{1,0:T(8,128)S(1)} concatenate(f32[256,64]{1,0:T(8,128)S(1)} %collective-permute-done, f32[256,2048]{1,0:T(8,128)} %param.1, f32[256,64]{1,0:T(8,128)S(1)} %collective-permute-done.1), dimensions={1} | concatenate | bytes 4456448 | tf_op jit(solution)/shard_map/concatenate | solution.py:28
  11.9 0.1 fusion.103
  12.0 4.5 %collective-permute-start.2 = (f32[64,2176]{1,0:T(8,128)S(1)}, f32[64,2176]{1,0:T(8,128)}, u32[]{:S(2)}, u32[]{:S(2)}) collective-permute-start(f32[64,2176]{1,0:T(8,128)S(1)} %get-tuple-element.11), channel_id=1, source_target_pairs={{0,2},{2,4},{4,6},{6,8},{8,10},{10,12},{12,14},{14,16},{16,18},{18... | collective-permute-start | bytes 1671176 | tf_op jit(solution)/shard_map/ppermute | solution.py:24
  16.6 1.9 %collective-permute-start.3 = (f32[64,2176]{1,0:T(8,128)S(1)}, f32[64,2176]{1,0:T(8,128)}, u32[]{:S(2)}, u32[]{:S(2)}) collective-permute-start(f32[64,2176]{1,0:T(8,128)S(1)} %get-tuple-element.12), channel_id=1, source_target_pairs={{2,0},{4,2},{6,4},{8,6},{10,8},{12,10},{14,12},{16,14},{18,16},{20... | collective-permute-start | bytes 1671176 | tf_op jit(solution)/shard_map/ppermute | solution.py:27
  18.6 10.4 %collective-permute-done.2 = f32[64,2176]{1,0:T(8,128)} collective-permute-done((f32[64,2176]{1,0:T(8,128)S(1)}, f32[64,2176]{1,0:T(8,128)}, u32[]{:S(2)}, u32[]{:S(2)}) %collective-permute-start.2) | collective-permute-done | bytes 557088 | tf_op jit(solution)/shard_map/ppermute | solution.py:24
  29.0 1.7 %collective-permute-done.3 = f32[64,2176]{1,0:T(8,128)} collective-permute-done((f32[64,2176]{1,0:T(8,128)S(1)}, f32[64,2176]{1,0:T(8,128)}, u32[]{:S(2)}, u32[]{:S(2)}) %collective-permute-start.3) | collective-permute-done | bytes 557088 | tf_op jit(solution)/shard_map/ppermute | solution.py:27
  30.7 1.7 %fusion = f32[384,2176]{1,0:T(8,128)S(1)} fusion(f32[64,2176]{1,0:T(8,128)} %collective-permute-done.3, f32[256,2176]{1,0:T(8,128)S(1)} %concatenate.6, f32[64,2176]{1,0:T(8,128)} %collective-permute-done.2, f32[2176]{0:T(1024)S(1)} %get-tuple-element.4, f32[2176]{0:T(1024)S(1)} %get-tuple-element.3, pred[384]{0:T(512)(128)(4,1)S(1)} %get-tuple-element.16, ...), kind=kLoop, calls=%fused_computation.2 | loop fusion | flops 3342336 | bytes 6702848 | tf_op jit(solution)/shard_map/jit(_where)/select_n | solution.py:85
  32.3 28.6 %add_maximum_fusion = (f32[256,2048]{1,0:T(8,128)}, f32[256,2048]{1,0:T(8,128)S(1)}, f32[256,2048]{1,0:T(8,128)S(1)}) fusion(f32[256]{0:T(256)S(1)} %sine_multiply_fusion, f32[384,2176]{1,0:T(8,128)S(1)} %fusion), kind=kLoop, calls=%fused_computation.127 | loop fusion | flops 72351744 | bytes 123732992 | tf_op jit(solution)/shard_map/max | solution.py:70
  60.9 4.6 %fusion.97 = (f32[1,256,2048]{2,1,0:T(8,128)S(1)}, f32[1,256,2048]{2,1,0:T(8,128)S(1)}, f32[256,2048]{1,0:T(8,128)}) fusion(f32[256,2048]{1,0:T(8,128)S(1)} %get-tuple-element.6, f32[256,2048]{1,0:T(8,128)S(1)} %get-tuple-element.7), kind=kLoop, calls=%fused_computation.133 | loop fusion | flops 4194304 | bytes 10485760 | tf_op jit(solution)/shard_map/stack | solution.py:73
  65.5 2.5 %pad_maximum_fusion = f32[2,256,2048]{2,1,0:T(8,128)} fusion(f32[1,256,2048]{2,1,0:T(8,128)S(1)} %get-tuple-element.9, f32[1,256,2048]{2,1,0:T(8,128)S(1)} %get-tuple-element.8), kind=kLoop, calls=%fused_computation | loop fusion | flops 1048576 | bytes 8388608 | tf_op jit(solution)/shard_map/stack | solution.py:73
  (3 shorter events, 0.1 us)
Async XLA Ops:
  1.7 4.4 %collective-permute-start.1 = (f32[256,64]{1,0:T(8,128)S(1)}, f32[256,64]{1,0:T(8,128)S(1)}, u32[]{:S(2)}, u32[]{:S(2)}) collective-permute-start(f32[256,64]{1,0:T(8,128)S(1)} %get-tuple-element.13), channel_id=1, source_target_pairs={{1,0},{0,1},{3,2},{2,3},{5,4},{4,5},{7,6},{6,7},{9,8},{8,9},{11,10... | collective-permute-start | bytes 196616 | tf_op jit(solution)/shard_map/ppermute | solution.py:27
  3.0 6.0 %collective-permute-start = (f32[256,64]{1,0:T(8,128)S(1)}, f32[256,64]{1,0:T(8,128)S(1)}, u32[]{:S(2)}, u32[]{:S(2)}) collective-permute-start(f32[256,64]{1,0:T(8,128)S(1)} %get-tuple-element.14), channel_id=1, source_target_pairs={{0,1},{1,0},{2,3},{3,2},{4,5},{5,4},{6,7},{7,6},{8,9},{9,8},{10,11... | collective-permute-start | bytes 196616 | tf_op jit(solution)/shard_map/ppermute | solution.py:24
  12.0 17.0 %collective-permute-start.2 = (f32[64,2176]{1,0:T(8,128)S(1)}, f32[64,2176]{1,0:T(8,128)}, u32[]{:S(2)}, u32[]{:S(2)}) collective-permute-start(f32[64,2176]{1,0:T(8,128)S(1)} %get-tuple-element.11), channel_id=1, source_target_pairs={{0,2},{2,4},{4,6},{6,8},{8,10},{10,12},{12,14},{14,16},{16,18},{18... | collective-permute-start | bytes 1671176 | tf_op jit(solution)/shard_map/ppermute | solution.py:24
  16.6 14.1 %collective-permute-start.3 = (f32[64,2176]{1,0:T(8,128)S(1)}, f32[64,2176]{1,0:T(8,128)}, u32[]{:S(2)}, u32[]{:S(2)}) collective-permute-start(f32[64,2176]{1,0:T(8,128)S(1)} %get-tuple-element.12), channel_id=1, source_target_pairs={{2,0},{4,2},{6,4},{8,6},{10,8},{12,10},{14,12},{16,14},{18,16},{20... | collective-permute-start | bytes 1671176 | tf_op jit(solution)/shard_map/ppermute | solution.py:27
where the time goes:
time: 68.3 us; the launch traced here: 68.1 us
  other arithmetic  37.4 us (55%)
  waiting for transfers between devices  17.8 us (26%)
  starting transfers between devices  7.99 us (12%)
  local copies, waits for them, and re-layouts  4.15 us (6%)
  between operations  0.7 us (1%)
    max x1, other arithmetic, terrain_shading(): jnp.maximum(LIGHT_EAST * facing_east + LIGHT_NORTH * facing_north + LIGHT...  28.6 us
    ppermute x2, waiting for transfers between devices, padded_2(): lax.ppermute(lax.slice_in_dim(block, block.shape[dim] - width, None, axis...  13.2 us
    another operation x2, other arithmetic, terrain_shading(): return (slope_angle, jnp.stack([facing_east, facing_north]), shading)  7.15 us
    ppermute x2, starting transfers between devices, padded_2(): lax.ppermute(lax.slice_in_dim(block, block.shape[dim] - width, None, axis...  4.76 us
    ppermute x2, waiting for transfers between devices, padded_2(): lax.ppermute(lax.slice_in_dim(block, 0, width, axis=dim), axis, backward)  4.61 us
    ppermute x2, starting transfers between devices, padded_2(): lax.ppermute(lax.slice_in_dim(block, 0, width, axis=dim), axis, backward)  3.23 us
    concatenate x1, local copies, waits for them, and re-layouts, padded_2(): block = jnp.concatenate([low, block, high], axis=dim)  2.97 us
    select_n x1, other arithmetic, pole_clamp(): return jnp.where(above, top_row, jnp.where(below, bottom_row, padded))  1.66 us
  transfers between devices with their start and end apart: 4, of which 4 were waited for; matrix products, arithmetic and copies ran while one was open for 0% of the time, Pallas kernels for 0%

commit v1 on v0

v1 whole, which is shorter than its diff:
```python
import functools
import math

import jax
import jax.numpy as jnp
from jax import lax
from jax.experimental import pallas as pl
from jax.experimental.pallas import tpu as pltpu
from jax.sharding import PartitionSpec as P

SCALES = 7
HALO = 64
LANES = 128
SUB = 8
GROUP = 4

LIGHT_UP = math.sqrt(0.5)
MESH = pl.DeviceIdType.MESH

ANGLE = (
    1.5707963068901982,
    -0.9999960003074525,
    0.7852630240552405,
    -0.6648577772093989,
    0.5764135907397322,
    -0.48061340102986794,
    0.3483872625788081,
    -0.19210392123613929,
    0.06787372952021542,
    -0.011162824266648386,
)


def row_pad(stride):
    return max(stride, SUB)


def kernel(rows, cols, z_ref, coef_ref, slope_ref, facing_ref, shade_ref, *scratch):
    lags, (zbuf, wsum, load_sem, send_sem, recv_sem, rim_send, rim_recv) = (
        scratch[:SCALES],
        scratch[SCALES:],
    )
    lat, lon = lax.axis_index("lat"), lax.axis_index("lon")
    n_lat, n_lon = lax.axis_size("lat"), lax.axis_size("lon")
    west, east = lax.rem(lon + n_lon - 1, n_lon), lax.rem(lon + 1, n_lon)
    strips = cols // LANES
    groups = strips // GROUP
    exists = (lat > 0, lat < n_lat - 1)
    neighbour = (lat - 1, lat + 1)
    lane = lax.broadcasted_iota(jnp.int32, (SUB, LANES), 1)

    edge_rows = (0, rows - HALO)
    loads = []
    for number, (start, count) in enumerate(
        ((0, HALO), (rows - HALO, HALO), (HALO, rows - 2 * HALO))
    ):
        load = pltpu.make_async_copy(
            z_ref.at[pl.ds(start, count), :],
            zbuf.at[pl.ds(HALO + start, count), pl.ds(LANES, cols)],
            load_sem.at[number],
        )
        load.start()
        loads.append(load)

    barrier = pltpu.get_barrier_semaphore()
    for side_lon in (west, east):
        pl.semaphore_signal(barrier, inc=1, device_id=(lat, side_lon), device_id_type=MESH)
    for side in range(2):

        @pl.when(exists[side])
        def _():
            for other in (lon, west, east):
                pl.semaphore_signal(
                    barrier, inc=1, device_id=(neighbour[side], other), device_id_type=MESH
                )

    pl.semaphore_wait(
        barrier, 2 + 3 * (exists[0].astype(jnp.int32) + exists[1].astype(jnp.int32))
    )

    bounds = [0] + [min(GROUP * k + 1, strips) for k in range(1, groups)] + [strips]

    def piece(number):
        if number == groups:
            return 0, LANES
        if number == groups + 1:
            return LANES + cols, LANES
        return LANES + bounds[number] * LANES, (bounds[number + 1] - bounds[number]) * LANES

    def lat_copy(side, number):
        start, width = piece(number)
        source_start, other = start, lon
        if number == groups:
            source_start, start, other = LANES, LANES + cols, west
        if number == groups + 1:
            source_start, start, other = cols, 0, east
        index = number
        if number == groups:
            index = groups + 1
        if number == groups + 1:
            index = groups
        target_row = HALO + rows if side == 0 else 0
        return pltpu.make_async_remote_copy(
            src_ref=zbuf.at[pl.ds(HALO + edge_rows[side], HALO), pl.ds(source_start, width)],
            dst_ref=zbuf.at[pl.ds(target_row, HALO), pl.ds(start, width)],
            send_sem=send_sem.at[side, number],
            recv_sem=recv_sem.at[1 - side, index],
            device_id=(neighbour[side], other),
            device_id_type=MESH,
        )

    def rim_copy(side):
        source_start, start, other = ((LANES, LANES + cols, west), (cols, 0, east))[side]
        return pltpu.make_async_remote_copy(
            src_ref=zbuf.at[pl.ds(HALO, rows), pl.ds(source_start, LANES)],
            dst_ref=zbuf.at[pl.ds(HALO, rows), pl.ds(start, LANES)],
            send_sem=rim_send.at[side],
            recv_sem=rim_recv.at[side],
            device_id=(lat, other),
            device_id_type=MESH,
        )

    order = [groups + 1] + list(range(groups)) + [groups]
    for side in range(2):
        loads[side].wait()

        @pl.when(exists[side])
        def _():
            for number in order:
                lat_copy(side, number).start()

    loads[2].wait()
    for side in range(2):
        rim_copy(side).start()

    def widen(first_row, count, octaves, group, with_centre):
        def step(index, carry):
            row = pl.multiple_of(first_row + index * SUB, SUB)
            column = pl.multiple_of(group * (GROUP * LANES), LANES)
            z = [
                zbuf[pl.ds(row, SUB), pl.ds(column + k * LANES, LANES)] for k in range(GROUP + 2)
            ]
            centre = [None] * GROUP
            for octave in octaves:
                stride = 2**octave
                scaled = [v * (1.0 / stride) for v in z] if octave else z
                ahead = [pltpu.roll(v, LANES - stride, 1) for v in scaled[1:]]
                if 2 * stride == LANES:
                    behind = [pltpu.roll(scaled[0], stride, 1)] + ahead[:-1]
                else:
                    behind = [pltpu.roll(v, stride, 1) for v in scaled[:-1]]
                store_row = pl.multiple_of(row - HALO + row_pad(stride), SUB)
                for k in range(GROUP):
                    plus = jnp.where(lane < LANES - stride, ahead[k], ahead[k + 1])
                    minus = jnp.where(lane >= stride, behind[k + 1], behind[k])
                    strip = group * GROUP + k
                    lags[octave][0, strip, pl.ds(store_row, SUB), :] = scaled[k + 1] + plus
                    lags[octave][1, strip, pl.ds(store_row, SUB), :] = scaled[k + 1] + minus
                    if with_centre:
                        term = plus - minus
                        centre[k] = term if centre[k] is None else centre[k] + term
            if with_centre:
                for k in range(GROUP):
                    wsum[group * GROUP + k, pl.ds(pl.multiple_of(row - HALO, SUB), SUB), :] = (
                        centre[k] + centre[k]
                    )
            return carry

        lax.fori_loop(0, count // SUB, step, 0)

    def shade(first_row, count, group):
        def step(index, carry):
            row = pl.multiple_of(first_row + index * SUB, SUB)
            coef = coef_ref[pl.ds(row, SUB), :]
            for k in range(GROUP):
                strip = group * GROUP + k
                down = up = None
                for octave in range(SCALES):
                    stride = 2**octave
                    lag = lags[octave]
                    north = pl.ds(row + (row_pad(stride) - stride), SUB)
                    south = pl.ds(row + (row_pad(stride) + stride), SUB)
                    a = lag[0, strip, south, :] - lag[1, strip, north, :]
                    b = lag[0, strip, north, :] - lag[1, strip, south, :]
                    down = a if down is None else down + a
                    up = b if up is None else up + b
                grad_east = (wsum[strip, pl.ds(row, SUB), :] + (down + up)) * coef
                grad_north = (up - down) * (1.0 / (8.0 * SCALES))
                squared = grad_east * grad_east + grad_north * grad_north
                inverse = lax.rsqrt(1.0 + squared)
                sine = squared * lax.rsqrt(jnp.maximum(squared, 1e-37)) * inverse
                ratio = jnp.full_like(inverse, ANGLE[-1])
                for term in ANGLE[-2::-1]:
                    ratio = ratio * inverse + term
                facing_east = -grad_east * inverse
                facing_north = -grad_north * inverse
                shading = jnp.maximum(
                    0.5 * (facing_north - facing_east) + LIGHT_UP * inverse, 0.0
                )
                place = (
                    pl.ds(row, SUB),
                    pl.ds(pl.multiple_of(group * (GROUP * LANES), LANES) + k * LANES, LANES),
                )
                slope_ref[place] = sine * ratio
                facing_ref[(0,) + place] = facing_east
                facing_ref[(1,) + place] = facing_north
                shade_ref[place] = shading
            return carry

        lax.fori_loop(0, count // SUB, step, 0)

    def inner(index, carry):
        group = lax.rem(index + 1, groups)

        @pl.when(index == max(groups - 2, 0))
        def _():
            for side in range(2):
                rim_copy(side).wait_recv()

        widen(HALO, rows, range(SCALES), group, True)
        shade(HALO, rows - 2 * HALO, group)
        return carry

    lax.fori_loop(0, groups, inner, 0)

    near = 1 - lax.rem(lat, 2)

    def outer(index, carry):
        side = jnp.where(index == 0, near, 1 - near)
        here = jnp.where(side == 0, lat > 0, lat < n_lat - 1)
        top = side == 0
        halo_row = pl.multiple_of(jnp.where(top, 0, HALO + rows), SUB)

        def wait_piece(number):
            start, width = piece(number)
            pltpu.make_async_remote_copy(
                src_ref=zbuf.at[pl.ds(halo_row, HALO), pl.ds(start, width)],
                dst_ref=zbuf.at[pl.ds(halo_row, HALO), pl.ds(start, width)],
                send_sem=send_sem.at[0, number],
                recv_sem=recv_sem.at[side, number],
                device_id=(lat, east),
                device_id_type=MESH,
            ).wait_recv()

        for pole in range(2):

            @pl.when(jnp.logical_and(jnp.logical_not(here), side == pole))
            def _():
                first = HALO if pole == 0 else HALO + rows - SUB
                pick = 0 if pole == 0 else SUB - 1
                fill = 0 if pole == 0 else HALO + rows

                def repeat(strip, carry):
                    column = pl.ds(pl.multiple_of(strip * LANES, LANES), LANES)
                    edge = zbuf[pl.ds(first, SUB), column][pick : pick + 1]
                    block = jnp.broadcast_to(edge, (SUB, LANES))
                    for k in range(HALO // SUB):
                        zbuf[pl.ds(fill + k * SUB, SUB), column] = block
                    return carry

                lax.fori_loop(0, strips + 2, repeat, 0)

        def one_group(group, carry):
            for k in range(groups):

                @pl.when(jnp.logical_and(here, group == k))
                def _():
                    wait_piece(k)
                    if k == 0:
                        wait_piece(groups)
                    if k == groups - 1:
                        wait_piece(groups + 1)

            reach = 0
            for octave in range(SCALES):
                stride = 2**octave
                if stride < SUB:
                    continue
                first = jnp.where(top, HALO - stride, HALO + rows + reach)
                octaves = range(SCALES) if reach == 0 else range(octave, SCALES)
                widen(first, stride - reach, octaves, group, False)
                reach = stride
            shade(jnp.where(top, 0, rows - HALO), HALO, group)
            return carry

        lax.fori_loop(0, groups, one_group, 0)
        return carry

    lax.fori_loop(0, 2, outer, 0)

    for side in range(2):
        rim_copy(side).wait_send()

        @pl.when(exists[side])
        def _():
            for number in order:
                lat_copy(side, number).wait_send()


def local(elevation):
    rows, cols = elevation.shape
    strips = cols // LANES
    groups = strips // GROUP
    total_rows = rows * lax.axis_size("lat")
    total_cols = cols * lax.axis_size("lon")
    position = lax.axis_index("lat") * rows + lax.iota(jnp.int32, rows)
    spacing = jnp.sin((position.astype(jnp.float32) + 0.5) * (math.pi / total_rows)) * (
        2.0 * total_rows / total_cols
    )
    coef = jnp.broadcast_to((1.0 / (8.0 * SCALES * spacing))[:, None], (rows, LANES))
    return tuple(
        pl.pallas_call(
            functools.partial(kernel, rows, cols),
            out_shape=(
                pltpu.VMEM((rows, cols), jnp.float32),
                pltpu.VMEM((2, rows, cols), jnp.float32),
                pltpu.VMEM((rows, cols), jnp.float32),
            ),
            in_specs=[
                pl.BlockSpec(memory_space=pl.ANY),
                pl.BlockSpec(memory_space=pltpu.VMEM),
            ],
            out_specs=tuple([pl.BlockSpec(memory_space=pltpu.VMEM)] * 3),
            scratch_shapes=[
                pltpu.VMEM((2, strips, rows + 2 * row_pad(2**k), LANES), jnp.float32)
                for k in range(SCALES)
            ]
            + [
                pltpu.VMEM((rows + 2 * HALO, cols + 2 * LANES), jnp.float32),
                pltpu.VMEM((strips, rows, LANES), jnp.float32),
                pltpu.SemaphoreType.DMA((3,)),
                pltpu.SemaphoreType.DMA((2, groups + 2)),
                pltpu.SemaphoreType.DMA((2, groups + 2)),
                pltpu.SemaphoreType.DMA((2,)),
                pltpu.SemaphoreType.DMA((2,)),
            ],
            compiler_params=pltpu.CompilerParams(
                collective_id=0, has_side_effects=True, vmem_limit_bytes=52 * 2**20
            ),
        )(elevation, coef)
    )


def solution(mesh):
    in_specs = (P("lat", "lon"),)
    out_specs = (P("lat", "lon"), P(None, "lat", "lon"), P("lat", "lon"))
    return jax.shard_map(local, mesh=mesh, in_specs=in_specs, out_specs=out_specs, check_vma=False)
```

time: 68.3 us -> 44.4 us (0.65)
  the two profiles are of different devices: /device:TPU:9 before, /device:TPU:0 now
where the time goes in v1:
time: 44.4 us; the launch traced here: 43.7 us
  Pallas kernels  37.6 us (85%)
  local copies, waits for them, and re-layouts  5.42 us (12%)
  between operations  0.64 us (1%)
    pallas_call x1, Pallas kernels, local(): pl.pallas_call(functools.partial(kernel, rows, cols), out_shape=(pltpu.VM...  37.6 us
    unnamed x3, local copies, waits for them, and re-layouts  4.65 us

profile of v1, /device:TPU:0, one launch (start us, length us, event | category | flops | bytes accessed | tf_op | source)
XLA Modules:
  0.0 43.7 jit_solution(12031084014041178686)
XLA Ops:
  0.7 0.8 %broadcast_in_dim.2.coef_ref = f32[256,128]{1,0:T(8,128)} broadcast(f32[256]{0:T(256)S(1)} %multiply_divide_fusion), dimensions={0} | broadcast | bytes 132096 | tf_op jit(solution)/shard_map/broadcast_in_dim | solution.py:310
  1.4 37.6 %shard_map.38 = (f32[256,2048]{1,0:T(8,128)S(1)}, f32[2,256,2048]{2,1,0:T(8,128)S(1)}, f32[256,2048]{1,0:T(8,128)S(1)}) custom-call(f32[256,2048]{1,0:T(8,128)} %z_ref.1, f32[256,128]{1,0:T(8,128)} %broadcast_in_dim.2.coef_ref), custom_call_target="tpu_custom_call" | custom-call | tf_op jit(solution)/shard_map/pallas_call | solution.py:312
  39.1 1.3 %copy.7 = f32[256,2048]{1,0:T(8,128)} copy(f32[256,2048]{1,0:T(8,128)S(1)} %get-tuple-element.3) | data formatting | bytes 4194304
  40.4 1.3 %copy.9 = f32[256,2048]{1,0:T(8,128)} copy(f32[256,2048]{1,0:T(8,128)S(1)} %get-tuple-element.5) | data formatting | bytes 4194304
  41.7 2.0 %copy.8 = f32[2,256,2048]{2,1,0:T(8,128)} copy(f32[2,256,2048]{2,1,0:T(8,128)S(1)} %get-tuple-element.4) | data formatting | bytes 8388608
  (1 shorter events, 0.0 us)

commit v2 on v1

v2 whole, which is shorter than its diff:
```python
import functools
import math

import jax
import jax.numpy as jnp
from jax import lax
from jax.experimental import pallas as pl
from jax.experimental.pallas import tpu as pltpu
from jax.sharding import PartitionSpec as P

SCALES = 7
HALO = 64
LANES = 128
SUB = 8
GROUP = 8

LIGHT_UP = math.sqrt(0.5)
MESH = pl.DeviceIdType.MESH

ANGLE = (
    1.5707963068901982,
    -0.9999960003074525,
    0.7852630240552405,
    -0.6648577772093989,
    0.5764135907397322,
    -0.48061340102986794,
    0.3483872625788081,
    -0.19210392123613929,
    0.06787372952021542,
    -0.011162824266648386,
)


def row_pad(stride):
    return max(stride, SUB)


def kernel(rows, cols, z_ref, coef_ref, slope_ref, facing_ref, shade_ref, *scratch):
    lags, (zbuf, wsum, load_sem, send_sem, recv_sem, rim_send, rim_recv) = (
        scratch[:SCALES],
        scratch[SCALES:],
    )
    lat, lon = lax.axis_index("lat"), lax.axis_index("lon")
    n_lat, n_lon = lax.axis_size("lat"), lax.axis_size("lon")
    west, east = lax.rem(lon + n_lon - 1, n_lon), lax.rem(lon + 1, n_lon)
    strips = cols // LANES
    groups = strips // GROUP
    exists = (lat > 0, lat < n_lat - 1)
    neighbour = (lat - 1, lat + 1)
    lane = lax.broadcasted_iota(jnp.int32, (SUB, LANES), 1)

    edge_rows = (0, rows - HALO)
    loads = []
    for number, (start, count) in enumerate(
        ((0, HALO), (rows - HALO, HALO), (HALO, rows - 2 * HALO))
    ):
        load = pltpu.make_async_copy(
            z_ref.at[pl.ds(start, count), :],
            zbuf.at[pl.ds(HALO + start, count), pl.ds(LANES, cols)],
            load_sem.at[number],
        )
        load.start()
        loads.append(load)

    barrier = pltpu.get_barrier_semaphore()
    for side_lon in (west, east):
        pl.semaphore_signal(barrier, inc=1, device_id=(lat, side_lon), device_id_type=MESH)
    for side in range(2):

        @pl.when(exists[side])
        def _():
            for other in (lon, west, east):
                pl.semaphore_signal(
                    barrier, inc=1, device_id=(neighbour[side], other), device_id_type=MESH
                )

    pl.semaphore_wait(
        barrier, 2 + 3 * (exists[0].astype(jnp.int32) + exists[1].astype(jnp.int32))
    )

    bounds = [0] + [min(GROUP * k + 1, strips) for k in range(1, groups)] + [strips]

    def piece(number):
        if number == groups:
            return 0, LANES
        if number == groups + 1:
            return LANES + cols, LANES
        return LANES + bounds[number] * LANES, (bounds[number + 1] - bounds[number]) * LANES

    def lat_copy(side, number):
        start, width = piece(number)
        source_start, other = start, lon
        if number == groups:
            source_start, start, other = LANES, LANES + cols, west
        if number == groups + 1:
            source_start, start, other = cols, 0, east
        index = number
        if number == groups:
            index = groups + 1
        if number == groups + 1:
            index = groups
        target_row = HALO + rows if side == 0 else 0
        return pltpu.make_async_remote_copy(
            src_ref=zbuf.at[pl.ds(HALO + edge_rows[side], HALO), pl.ds(source_start, width)],
            dst_ref=zbuf.at[pl.ds(target_row, HALO), pl.ds(start, width)],
            send_sem=send_sem.at[side, number],
            recv_sem=recv_sem.at[1 - side, index],
            device_id=(neighbour[side], other),
            device_id_type=MESH,
        )

    def rim_copy(side):
        source_start, start, other = ((LANES, LANES + cols, west), (cols, 0, east))[side]
        return pltpu.make_async_remote_copy(
            src_ref=zbuf.at[pl.ds(HALO, rows), pl.ds(source_start, LANES)],
            dst_ref=zbuf.at[pl.ds(HALO, rows), pl.ds(start, LANES)],
            send_sem=rim_send.at[side],
            recv_sem=rim_recv.at[side],
            device_id=(lat, other),
            device_id_type=MESH,
        )

    order = [groups + 1] + list(range(groups)) + [groups]
    for side in range(2):
        loads[side].wait()

        @pl.when(exists[side])
        def _():
            for number in order:
                lat_copy(side, number).start()

    loads[2].wait()
    for side in range(2):
        rim_copy(side).start()

    def column_of(group):
        return pl.multiple_of(group * (GROUP * LANES), LANES)

    def rotate(row, octaves, group):
        column = column_of(group)
        z = [zbuf[pl.ds(row, SUB), pl.ds(column + k * LANES, LANES)] for k in range(GROUP + 2)]
        found = []
        for octave in octaves:
            stride = 2**octave
            scaled = [v * (1.0 / stride) for v in z] if octave else z
            ahead = [pltpu.roll(v, LANES - stride, 1) for v in scaled[1:]]
            if 2 * stride == LANES:
                behind = [pltpu.roll(scaled[0], stride, 1)] + ahead[:-1]
            else:
                behind = [pltpu.roll(v, stride, 1) for v in scaled[:-1]]
            found.append((octave, scaled, ahead, behind))
        return found

    def store(row, found, group, with_centre):
        centre = [None] * GROUP
        for octave, scaled, ahead, behind in found:
            stride = 2**octave
            store_row = pl.multiple_of(row - HALO + row_pad(stride), SUB)
            for k in range(GROUP):
                plus = jnp.where(lane < LANES - stride, ahead[k], ahead[k + 1])
                minus = jnp.where(lane >= stride, behind[k + 1], behind[k])
                strip = group * GROUP + k
                lags[octave][0, strip, pl.ds(store_row, SUB), :] = scaled[k + 1] + plus
                lags[octave][1, strip, pl.ds(store_row, SUB), :] = scaled[k + 1] + minus
                if with_centre:
                    term = plus - minus
                    centre[k] = term if centre[k] is None else centre[k] + term
        if with_centre:
            for k in range(GROUP):
                wsum[group * GROUP + k, pl.ds(pl.multiple_of(row - HALO, SUB), SUB), :] = (
                    centre[k] + centre[k]
                )

    def shade(row, group):
        coef = coef_ref[pl.ds(row, SUB), :]
        for k in range(GROUP):
            strip = group * GROUP + k
            down = up = None
            for octave in range(SCALES):
                stride = 2**octave
                lag = lags[octave]
                north = pl.ds(row + (row_pad(stride) - stride), SUB)
                south = pl.ds(row + (row_pad(stride) + stride), SUB)
                a = lag[0, strip, south, :] - lag[1, strip, north, :]
                b = lag[0, strip, north, :] - lag[1, strip, south, :]
                down = a if down is None else down + a
                up = b if up is None else up + b
            grad_east = (wsum[strip, pl.ds(row, SUB), :] + (down + up)) * coef
            grad_north = (up - down) * (1.0 / (8.0 * SCALES))
            squared = grad_east * grad_east + grad_north * grad_north
            inverse = lax.rsqrt(1.0 + squared)
            sine = squared * lax.rsqrt(jnp.maximum(squared, 1e-37)) * inverse
            ratio = jnp.full_like(inverse, ANGLE[-1])
            for term in ANGLE[-2::-1]:
                ratio = ratio * inverse + term
            facing_east = -grad_east * inverse
            facing_north = -grad_north * inverse
            shading = jnp.maximum(0.5 * (facing_north - facing_east) + LIGHT_UP * inverse, 0.0)
            place = (pl.ds(row, SUB), pl.ds(column_of(group) + k * LANES, LANES))
            slope_ref[place] = sine * ratio
            facing_ref[(0,) + place] = facing_east
            facing_ref[(1,) + place] = facing_north
            shade_ref[place] = shading

    near = 1 - lax.rem(lat, 2)
    far = 1 - near
    near_top = near == 0
    far_exists = jnp.where(near_top, exists[1], exists[0])

    def row_at(step):
        return pl.multiple_of(jnp.where(near_top, step * SUB, rows - SUB - step * SUB), SUB)

    def halo_row(side):
        return pl.multiple_of(jnp.where(side == 0, 0, HALO + rows), SUB)

    def wait_piece(side, number):
        start, width = piece(number)
        here = zbuf.at[pl.ds(halo_row(side), HALO), pl.ds(start, width)]
        pltpu.make_async_remote_copy(
            src_ref=here,
            dst_ref=here,
            send_sem=send_sem.at[0, number],
            recv_sem=recv_sem.at[side, number],
            device_id=(lat, east),
            device_id_type=MESH,
        ).wait_recv()

    def widen_halo(side, group):
        for distance in range(0, HALO, SUB):
            row = pl.multiple_of(
                jnp.where(side == 0, HALO - SUB - distance, HALO + rows + distance), SUB
            )
            octaves = [k for k in range(SCALES) if row_pad(2**k) > distance]
            store(row, rotate(row, octaves, group), group, False)

    ahead_steps = HALO // SUB + 1
    steps = rows // SUB

    def inner(index, carry):
        group = lax.rem(index + 1, groups)

        @pl.when(index == max(groups - 2, 0))
        def _():
            for side in range(2):
                rim_copy(side).wait_recv()

        def alone(step, carry):
            row = row_at(step) + HALO
            store(row, rotate(row, range(SCALES), group), group, True)
            return carry

        lax.fori_loop(0, ahead_steps, alone, 0)

        @pl.when(index == 0)
        def _():
            for number in order:
                wait_piece(near, number)

        widen_halo(near, group)

        def both(step, carry):
            row = row_at(step + ahead_steps) + HALO
            found = rotate(row, range(SCALES), group)
            shade(row_at(step), group)
            store(row, found, group, True)
            return carry

        lax.fori_loop(0, steps - ahead_steps, both, 0)
        return carry

    lax.fori_loop(0, groups, inner, 0)

    for pole in range(2):

        @pl.when(jnp.logical_and(jnp.logical_not(far_exists), far == pole))
        def _():
            first = HALO if pole == 0 else HALO + rows - SUB
            pick = 0 if pole == 0 else SUB - 1
            fill = 0 if pole == 0 else HALO + rows

            def repeat(strip, carry):
                column = pl.ds(pl.multiple_of(strip * LANES, LANES), LANES)
                edge = zbuf[pl.ds(first, SUB), column][pick : pick + 1]
                block = jnp.broadcast_to(edge, (SUB, LANES))
                for k in range(HALO // SUB):
                    zbuf[pl.ds(fill + k * SUB, SUB), column] = block
                return carry

            lax.fori_loop(0, strips + 2, repeat, 0)

    def last(group, carry):
        for k in range(groups):

            @pl.when(jnp.logical_and(far_exists, group == k))
            def _():
                wait_piece(far, k)
                if k == 0:
                    wait_piece(far, groups)
                if k == groups - 1:
                    wait_piece(far, groups + 1)

        widen_halo(far, group)

        def finish(step, carry):
            shade(row_at(step + steps - ahead_steps), group)
            return carry

        lax.fori_loop(0, ahead_steps, finish, 0)
        return carry

    lax.fori_loop(0, groups, last, 0)

    for side in range(2):
        rim_copy(side).wait_send()

        @pl.when(exists[side])
        def _():
            for number in order:
                lat_copy(side, number).wait_send()


def local(elevation):
    rows, cols = elevation.shape
    strips = cols // LANES
    groups = strips // GROUP
    total_rows = rows * lax.axis_size("lat")
    total_cols = cols * lax.axis_size("lon")
    position = lax.axis_index("lat") * rows + lax.iota(jnp.int32, rows)
    spacing = jnp.sin((position.astype(jnp.float32) + 0.5) * (math.pi / total_rows)) * (
        2.0 * total_rows / total_cols
    )
    coef = jnp.broadcast_to((1.0 / (8.0 * SCALES * spacing))[:, None], (rows, LANES))
    return tuple(
        pl.pallas_call(
            functools.partial(kernel, rows, cols),
            out_shape=(
                pltpu.VMEM((rows, cols), jnp.float32),
                pltpu.VMEM((2, rows, cols), jnp.float32),
                pltpu.VMEM((rows, cols), jnp.float32),
            ),
            in_specs=[
                pl.BlockSpec(memory_space=pl.ANY),
                pl.BlockSpec(memory_space=pltpu.VMEM),
            ],
            out_specs=tuple([pl.BlockSpec(memory_space=pltpu.VMEM)] * 3),
            scratch_shapes=[
                pltpu.VMEM((2, strips, rows + 2 * row_pad(2**k), LANES), jnp.float32)
                for k in range(SCALES)
            ]
            + [
                pltpu.VMEM((rows + 2 * HALO, cols + 2 * LANES), jnp.float32),
                pltpu.VMEM((strips, rows, LANES), jnp.float32),
                pltpu.SemaphoreType.DMA((3,)),
                pltpu.SemaphoreType.DMA((2, groups + 2)),
                pltpu.SemaphoreType.DMA((2, groups + 2)),
                pltpu.SemaphoreType.DMA((2,)),
                pltpu.SemaphoreType.DMA((2,)),
            ],
            compiler_params=pltpu.CompilerParams(
                collective_id=0, has_side_effects=True, vmem_limit_bytes=52 * 2**20
            ),
        )(elevation, coef)
    )


def solution(mesh):
    in_specs = (P("lat", "lon"),)
    out_specs = (P("lat", "lon"), P(None, "lat", "lon"), P("lat", "lon"))
    return jax.shard_map(local, mesh=mesh, in_specs=in_specs, out_specs=out_specs, check_vma=False)
```

time: 44.4 us -> 39.2 us (0.88); the launches traced: 43.7 us -> 39 us
  Pallas kernels: 37.6 us -> 32.9 us
    pallas_call x1, Pallas kernels: 37.6 us -> 32.9 us  [local(): pl.pallas_call(functools.partial(kernel, rows, cols), out_shape=(pltpu.VM...]
where the time goes in v2:
time: 39.2 us; the launch traced here: 39 us
  Pallas kernels  32.9 us (84%)
  local copies, waits for them, and re-layouts  5.42 us (14%)
  between operations  0.64 us (2%)
    pallas_call x1, Pallas kernels, local(): pl.pallas_call(functools.partial(kernel, rows, cols), out_shape=(pltpu.VM...  32.9 us
    unnamed x3, local copies, waits for them, and re-layouts  4.65 us

profile of v2, /device:TPU:0, one launch (start us, length us, event | category | flops | bytes accessed | tf_op | source)
XLA Modules:
  0.0 39.0 jit_solution(9922513401675577027)
XLA Ops:
  0.7 0.8 %broadcast_in_dim.2.coef_ref = f32[256,128]{1,0:T(8,128)} broadcast(f32[256]{0:T(256)S(1)} %multiply_divide_fusion), dimensions={0} | broadcast | bytes 132096 | tf_op jit(solution)/shard_map/broadcast_in_dim | solution.py:332
  1.4 32.9 %shard_map.38 = (f32[256,2048]{1,0:T(8,128)S(1)}, f32[2,256,2048]{2,1,0:T(8,128)S(1)}, f32[256,2048]{1,0:T(8,128)S(1)}) custom-call(f32[256,2048]{1,0:T(8,128)} %z_ref.1, f32[256,128]{1,0:T(8,128)} %broadcast_in_dim.2.coef_ref), custom_call_target="tpu_custom_call" | custom-call | tf_op jit(solution)/shard_map/pallas_call | solution.py:334
  34.3 1.3 %copy.7 = f32[256,2048]{1,0:T(8,128)} copy(f32[256,2048]{1,0:T(8,128)S(1)} %get-tuple-element.3) | data formatting | bytes 4194304
  35.7 1.3 %copy.9 = f32[256,2048]{1,0:T(8,128)} copy(f32[256,2048]{1,0:T(8,128)S(1)} %get-tuple-element.5) | data formatting | bytes 4194304
  37.0 2.0 %copy.8 = f32[2,256,2048]{2,1,0:T(8,128)} copy(f32[2,256,2048]{2,1,0:T(8,128)S(1)} %get-tuple-element.4) | data formatting | bytes 8388608
  (1 shorter events, 0.0 us)

commit v3 on v2

--- a/solution.py
+++ b/solution.py
@@ -35,8 +35,8 @@
     return max(stride, SUB)
 
 
-def kernel(rows, cols, z_ref, coef_ref, slope_ref, facing_ref, shade_ref, *scratch):
-    lags, (zbuf, wsum, load_sem, send_sem, recv_sem, rim_send, rim_recv) = (
+def kernel(rows, cols, z_ref, slope_ref, facing_ref, shade_ref, *scratch):
+    lags, (zbuf, wsum, coef_ref, load_sem, send_sem, recv_sem, rim_send, rim_recv) = (
         scratch[:SCALES],
         scratch[SCALES:],
     )
@@ -73,6 +73,15 @@
                 pl.semaphore_signal(
                     barrier, inc=1, device_id=(neighbour[side], other), device_id_type=MESH
                 )
+
+    total_rows = rows * n_lat
+    total_cols = cols * n_lon
+    for start in range(0, rows, SUB):
+        position = lat * rows + start + lax.broadcasted_iota(jnp.int32, (SUB, LANES), 0)
+        spacing = jnp.sin((position.astype(jnp.float32) + 0.5) * (math.pi / total_rows)) * (
+            2.0 * total_rows / total_cols
+        )
+        coef_ref[pl.ds(start, SUB), :] = 1.0 / (8.0 * SCALES * spacing)
 
     pl.semaphore_wait(
         barrier, 2 + 3 * (exists[0].astype(jnp.int32) + exists[1].astype(jnp.int32))
@@ -323,13 +332,6 @@
     rows, cols = elevation.shape
     strips = cols // LANES
     groups = strips // GROUP
-    total_rows = rows * lax.axis_size("lat")
-    total_cols = cols * lax.axis_size("lon")
-    position = lax.axis_index("lat") * rows + lax.iota(jnp.int32, rows)
-    spacing = jnp.sin((position.astype(jnp.float32) + 0.5) * (math.pi / total_rows)) * (
-        2.0 * total_rows / total_cols
-    )
-    coef = jnp.broadcast_to((1.0 / (8.0 * SCALES * spacing))[:, None], (rows, LANES))
     return tuple(
         pl.pallas_call(
             functools.partial(kernel, rows, cols),
@@ -340,7 +342,6 @@
             ),
             in_specs=[
                 pl.BlockSpec(memory_space=pl.ANY),
-                pl.BlockSpec(memory_space=pltpu.VMEM),
             ],
             out_specs=tuple([pl.BlockSpec(memory_space=pltpu.VMEM)] * 3),
             scratch_shapes=[
@@ -350,6 +351,7 @@
             + [
                 pltpu.VMEM((rows + 2 * HALO, cols + 2 * LANES), jnp.float32),
                 pltpu.VMEM((strips, rows, LANES), jnp.float32),
+                pltpu.VMEM((rows, LANES), jnp.float32),
                 pltpu.SemaphoreType.DMA((3,)),
                 pltpu.SemaphoreType.DMA((2, groups + 2)),
                 pltpu.SemaphoreType.DMA((2, groups + 2)),
@@ -359,7 +361,7 @@
             compiler_params=pltpu.CompilerParams(
                 collective_id=0, has_side_effects=True, vmem_limit_bytes=52 * 2**20
             ),
-        )(elevation, coef)
+        )(elevation)
     )
 
 

time: 39.2 us -> 37.5 us (0.957)
  Pallas kernels: 32.9 us -> 32 us
  local copies, waits for them, and re-layouts: 5.42 us -> 4.65 us
    pallas_call x1, Pallas kernels: 32.9 us -> 32 us  [local(): pl.pallas_call(functools.partial(kernel, rows, cols), out_shape=(pltpu.VM...]
    broadcast_in_dim x1 -> x0, local copies, waits for them, and re-layouts: 0.77 us -> none  [local(): jnp.broadcast_to((1.0 / (8.0 * SCALES * spacing))[:, None], (rows, LANES))]
where the time goes in v3:
time: 37.5 us; the launch traced here: 37.3 us
  Pallas kernels  32 us (85%)
  local copies, waits for them, and re-layouts  4.65 us (12%)
  between operations  0.64 us (2%)
    pallas_call x1, Pallas kernels, local(): pl.pallas_call(functools.partial(kernel, rows, cols), out_shape=(pltpu.VM...  32 us
    unnamed x3, local copies, waits for them, and re-layouts  4.65 us

profile of v3, /device:TPU:0, one launch (start us, length us, event | category | flops | bytes accessed | tf_op | source)
XLA Modules:
  0.0 37.3 jit_solution(15160389149323308299)
XLA Ops:
  0.6 32.0 %shard_map.38 = (f32[256,2048]{1,0:T(8,128)S(1)}, f32[2,256,2048]{2,1,0:T(8,128)S(1)}, f32[256,2048]{1,0:T(8,128)S(1)}) custom-call(f32[256,2048]{1,0:T(8,128)} %z_ref.1), custom_call_target="tpu_custom_call" | custom-call | tf_op jit(solution)/shard_map/pallas_call | solution.py:336
  32.7 1.3 %copy.7 = f32[256,2048]{1,0:T(8,128)} copy(f32[256,2048]{1,0:T(8,128)S(1)} %get-tuple-element.3) | data formatting | bytes 4194304
  34.0 1.3 %copy.9 = f32[256,2048]{1,0:T(8,128)} copy(f32[256,2048]{1,0:T(8,128)S(1)} %get-tuple-element.5) | data formatting | bytes 4194304
  35.3 2.0 %copy.8 = f32[2,256,2048]{2,1,0:T(8,128)} copy(f32[2,256,2048]{2,1,0:T(8,128)S(1)} %get-tuple-element.4) | data formatting | bytes 8388608
